TPU v7x, 32 devices: a whole 2x2x4 slice. The times are simulated.
32 devices in a mesh: blk: 32 (over z, y, x, core).
Axes of the slice: x: 2, y: 2, z: 4, core: 2. Of those that a mesh axis runs over, the one named last changes fastest.
Arguments:
- wannier: bfloat16 [64, 110592], P('blk'), may hold values from -6 to 6
- pairs: int32 [32, 2, 1, 6], P('blk'), may hold values from 0 to 24, as said below
Outputs:
- exchange_image: bfloat16 [64, 110592], P('blk')
Inputs may be any that keep to these rules, and one draw needn't show every extreme that they name: `pairs`: columns 0 and 1 lie in 0..1, columns 2 to 4 in 0..24, column 5 is 0 or 1; some device has all 1 slots live in every step.
All inputs are finite; a program needn't handle non-finite values.
Results may differ from a plain program's by a relative error of at most 0.00125.
Values may be sent and summed in bfloat16 or wider, within the bound.
No kernel may reach another device: no remote copies, remote signals or barrier semaphores. Data moves between devices by JAX's collectives and lax.ppermute only.
A program may use at most 64 MiB of HBM per device.

v0:
```python
import functools

import jax
import jax.numpy as jnp
import numpy as np
from jax import lax
from jax.experimental import pallas as pl
from jax.experimental.pallas import tpu as pltpu
from jax.sharding import PartitionSpec as P


LANES = 128
VMEM_BYTES = 20 * 1024 * 1024
PREP_BYTES = 64380928
PREP_CHUNKS = 4


class Plan:
    def __init__(self, points):
        self.g = g = round(points ** (1.0 / 3.0))
        assert g**3 == points and (g * g) % (2 * LANES) == 0 and g % 16 == 0
        self.modes = 2 * g
        assert self.modes <= LANES
        self.tiles = g * g // LANES
        self.rows = points // LANES
        half = g // 2
        self.pad = -(-(half * (g * g + g + 1) // LANES + 1) // 8) * 8


def split(x):
    hi = x.astype(jnp.bfloat16)
    lo = (x - hi.astype(jnp.float32)).astype(jnp.bfloat16)
    return hi, lo


def dot(a, b):
    return jnp.dot(a, b, preferred_element_type=jnp.float32)


def sine_table(shape, modes, row_end, lane_end):
    row = lax.broadcasted_iota(jnp.int32, shape, 0)
    lane = lax.broadcasted_iota(jnp.int32, shape, 1)
    period = 2 * (modes + 1)
    product = ((row + 1) * (lane + 1)).astype(jnp.float32)
    turns = jnp.floor((product + 0.5) * (1.0 / period))
    angle = (product - turns * period) * (np.pi / (modes + 1))
    sine = jnp.sin(angle) * np.sqrt(2.0 / (modes + 1.0))
    return jnp.where((row < row_end) & (lane < lane_end), sine, 0.0)


def tables_kernel(plan, start_ref, first_ref, last_ref, end_ref, ratio_ref):
    g, m = plan.g, plan.modes
    half = LANES // 2
    shape = (m, LANES)
    step = np.pi / (m + 1)
    row = lax.broadcasted_iota(jnp.int32, shape, 0).astype(jnp.float32)
    lane = lax.broadcasted_iota(jnp.int32, shape, 1).astype(jnp.float32)
    mu = 4.0 * (jnp.sin((row + 1.0) * (0.5 * step)) ** 2 + jnp.sin((lane + 1.0) * (0.5 * step)) ** 2)
    small = jnp.ones_like(mu)
    for j in range(g):
        before = small
        total = mu + small
        ratio = 1.0 / (1.0 + total)
        small = total * ratio
        if j == g - 1:
            ratio = 1.0 / (mu + before + small)
        ratio_ref[j] = ratio
    hi, lo = split(sine_table((m, LANES), m, m, g)[:, :g])
    first_ref[...] = jnp.concatenate([hi, hi, lo], axis=1)
    hi, lo = split(sine_table((g, LANES), m, g, m))
    gap = jnp.zeros((half - g, 2 * LANES), jnp.bfloat16)
    wide = jnp.concatenate([hi, lo], axis=1)
    start_ref[...] = jnp.concatenate([wide, gap, wide, gap], axis=0)
    end_ref[...] = jnp.concatenate(
        [jnp.concatenate([hi, hi], axis=1), jnp.concatenate([lo, lo], axis=1)], axis=0
    )
    hi, lo = hi[:, :m], lo[:, :m]
    last_ref[...] = jnp.concatenate(
        [jnp.concatenate([hi, hi], axis=1), jnp.concatenate([lo, lo], axis=1)], axis=0
    )


def prepare_kernel(plan, chunks, e_hbm, raw_hbm, w_ref, o1_ref, o2_ref, e_ref, raw_ref, both, sems):
    rows = plan.rows // chunks
    copies = [
        pltpu.make_async_copy(
            raw_hbm.at[pl.ds(2 * rows * at, 2 * rows)], raw_ref.at[pl.ds(2 * rows * at, 2 * rows)], sems.at[at]
        )
        for at in range(chunks)
    ]
    copies.append(pltpu.make_async_copy(e_hbm, e_ref, sems.at[chunks]))
    for copy in copies[-1:] + copies[:-1]:
        copy.start()
    copies[-1].wait()
    first = e_ref[0, 0, 0, 0] == 0
    second = e_ref[0, 1, 0, 0] == 0
    for at in range(chunks):
        copies[at].wait()
        here = pl.ds(rows * at, rows)
        both[pl.ds(2 * rows * at, 2 * rows), :] = raw_ref[pl.ds(2 * rows * at, 2 * rows), :].astype(jnp.float32)
        f0, f1 = [both[pl.ds(2 * rows * at + f, rows, stride=2), :] for f in range(2)]
        w_ref[0, here, :] = f0.astype(jnp.bfloat16)
        w_ref[1, here, :] = f1.astype(jnp.bfloat16)
        o1_ref[here, :] = jnp.where(first, f0, f1).astype(jnp.bfloat16)
        o2_ref[here, :] = jnp.where(second, f0, f1).astype(jnp.bfloat16)


def pick_kernel(step, e_ref, w_ref, out_ref):
    out_ref[...] = w_ref[e_ref[0, step, 0, 1]]


def solve_kernel(plan, role, step, *refs):
    owner = role.startswith("visiting")
    (e_ref, w_ref, x_ref, start_ref, first_ref, last_ref, end_ref, ratio_ref) = refs[:8]
    refs = refs[8:]
    if role == "visiting_sum":
        (other_e_ref, other_ref), refs = refs[:2], refs[2:]
    if role == "last":
        (partial_ref, other_ref), refs = refs[:2], refs[2:]
    out_ref, a_pad, b_pad, b_sh, rho_t, x_hi, x_lo, z, y_hi, y_lo, v = refs[:11]
    both = refs[11] if role == "last" else None
    g, m = plan.g, plan.modes
    r_at = e_ref[0, step, 0, 0]
    v_at = e_ref[0, step, 0, 1]
    ox = e_ref[0, step, 0, 2]
    oy = e_ref[0, step, 0, 3]
    oz = e_ref[0, step, 0, 4]
    live = e_ref[0, step, 0, 5].astype(jnp.float32)
    shift = ox * (g * g) + oy * g + oz
    down = lax.shift_right_logical(shift, 7)
    roll = shift & (LANES - 1)

    if owner:
        a_pad[: plan.rows, :] = x_ref[...].astype(jnp.float32)
        b_pad[plan.pad :, :] = w_ref[v_at].astype(jnp.float32)
    else:
        a_pad[: plan.rows, :] = w_ref[r_at].astype(jnp.float32)
        b_pad[plan.pad :, :] = x_ref[...].astype(jnp.float32)
    b_pad[: plan.pad, :] = jnp.zeros((plan.pad, LANES), jnp.float32)

    lane = lax.broadcasted_iota(jnp.int32, (8, LANES), 1)

    def j_and_k(t):
        flat = (lane + t * LANES).astype(jnp.float32)
        j = jnp.floor((flat + 0.5) * (1.0 / g))
        return j.astype(jnp.int32), (flat - j * g).astype(jnp.int32)

    def tall(x):
        return jnp.concatenate([x] * (g // 8), axis=0)

    def moved(ref, start, amount):
        return pltpu.roll(ref[pl.ds(start, g, stride=plan.tiles), :], amount, 1)

    from_before = tall(lane < roll)
    parts = 3
    js = g // parts
    tiles = plan.tiles // parts
    assert g % parts == 0 and js % 2 == 0 and plan.tiles % parts == 0 and tiles % 2 == 0
    last_rolled = [moved(b_pad, plan.pad - 1 - down, roll)]
    gap = jnp.zeros((LANES // 2 - g, LANES), jnp.bfloat16)

    def shift_and_start(part):
        for t in range(part * tiles, (part + 1) * tiles):
            before = last_rolled[0]
            here = moved(b_pad, plan.pad + t - down, roll)
            j, k = j_and_k(t)
            valid = tall((j >= oy) & (k >= oz))
            b = jnp.where(valid, jnp.where(from_before, before, here), 0.0)
            last_rolled[0] = here
            if not owner:
                b_sh[t] = b
            hi, lo = split(a_pad[pl.ds(t, g, stride=plan.tiles), :] * b)
            rho_t[pl.ds(t * LANES, LANES), :] = jnp.concatenate([hi, gap, lo, gap], axis=0).T
            if t % 2:
                rows = pl.ds((t - 1) * LANES, 2 * LANES)
                x = dot(rho_t[rows, :], start_ref[...])
                x_hi[rows, :], x_lo[rows, :] = split(x[:, :LANES] + x[:, LANES:])

    def beside(ref, j, rows):
        return jnp.concatenate([ref[pl.ds(j * rows, rows), :], ref[pl.ds((j + 1) * rows, rows), :]], axis=1)

    def first(part):
        for j in range(part * js, (part + 1) * js, 2):
            hi, lo = beside(x_hi, j, g), beside(x_lo, j, g)
            x = dot(first_ref[...], jnp.concatenate([hi, lo, hi], axis=0))
            z[j], z[j + 1] = x[:, :LANES], x[:, LANES:]

    swept = [None]

    def sweep_up(part):
        w = swept[0]
        for j in range(part * js, (part + 1) * js):
            w = z[j] if j == 0 else z[j] + ratio_ref[j - 1] * w
            z[j] = w
        swept[0] = w

    def sweep_down(part):
        y = swept[0]
        for j in reversed(range(part * js, (part + 1) * js)):
            y = ratio_ref[j] * (z[j] + y)
            y_hi[pl.ds(j * m, m), :], y_lo[pl.ds(j * m, m), :] = split(y)
        swept[0] = y

    def last(part):
        for j in reversed(range(part * js, (part + 1) * js, 2)):
            x = dot(last_ref[...], jnp.concatenate([beside(y_hi, j, m), beside(y_lo, j, m)], axis=0))
            hi, lo = split(x[:g] + x[g:])
            for side in range(2):
                rows = pl.ds((j + side) * g, g)
                lanes = slice(side * LANES, (side + 1) * LANES)
                v[rows, pl.ds(0, LANES)] = hi[:, lanes]
                v[rows, pl.ds(LANES, LANES)] = lo[:, lanes]

    def end(part):
        for pair in range(part * tiles // 2, (part + 1) * tiles // 2):
            pieces = lax.dot_general(
                end_ref[...],
                v[pl.ds(pair * 2 * LANES, 2 * LANES), :],
                (((1,), (1,)), ((), ())),
                preferred_element_type=jnp.float32,
            )
            phi2 = (pieces[:g] + pieces[g:]) * live
            for side in range(2):
                t = 2 * pair + side
                phi = phi2[:, side * LANES : (side + 1) * LANES]
                if owner:
                    b_pad[pl.ds(t, g, stride=plan.tiles), :] = phi * a_pad[pl.ds(t, g, stride=plan.tiles), :]
                elif role == "resident":
                    out_ref[t] = phi * b_sh[t]
                else:
                    own, other = phi * b_sh[t], other_ref[t]
                    other_at = e_ref[0, 0, 0, 0]
                    for f in range(2):
                        total = partial_ref[f, t]
                        total = total + jnp.where(other_at == f, other, 0.0) + jnp.where(r_at == f, own, 0.0)
                        both[pl.ds(2 * t + f, g, stride=2 * plan.tiles), :] = total

    for at in range(parts + 2):
        if at < parts:
            shift_and_start(at)
        if 0 <= at - 1 < parts:
            first(at - 1)
        if 0 <= at - 2 < parts:
            sweep_up(at - 2)
    swept[0] = jnp.zeros((m, LANES), jnp.float32)
    if owner:
        b_pad[plan.rows :, :] = jnp.zeros((plan.pad, LANES), jnp.float32)
    for at in range(parts + 2):
        if at < parts:
            sweep_down(parts - 1 - at)
        if 0 <= at - 1 < parts:
            last(parts - at)
        if 0 <= at - 2 < parts:
            end(parts + 1 - at)

    if owner:
        back = (LANES - roll) & (LANES - 1)
        from_here = tall(lane < LANES - roll)
        here = moved(b_pad, down, back)
        for t in range(plan.tiles):
            after = moved(b_pad, t + 1 + down, back)
            j, k = j_and_k(t)
            valid = tall((j < g - oy) & (k < g - oz))
            term = jnp.where(valid, jnp.where(from_here, here, after), 0.0)
            here = after
            if role == "visiting":
                out_ref[t] = term
                continue
            other, other_at = other_ref[t], other_e_ref[0, 0, 0, 1]
            for f in range(2):
                out_ref[f, t] = jnp.where(other_at == f, other, 0.0) + jnp.where(v_at == f, term, 0.0)
    if role == "last":
        out_ref[...] = both[...].astype(jnp.bfloat16)


def smem():
    return pl.BlockSpec(memory_space=pltpu.SMEM)


def vmem():
    return pl.BlockSpec(memory_space=pltpu.VMEM)


def params():
    return pltpu.CompilerParams(vmem_limit_bytes=VMEM_BYTES)


def cost(flops, size):
    return pl.CostEstimate(flops=flops, bytes_accessed=size, transcendentals=0)


def pick(step, e, w):
    return pl.pallas_call(
        functools.partial(pick_kernel, step),
        out_shape=jax.ShapeDtypeStruct(w.shape[1:], w.dtype),
        in_specs=[smem(), vmem()],
        out_specs=vmem(),
        compiler_params=params(),
        cost_estimate=cost(10**6, 10**6),
        name="pick",
    )(e, w)


def prepare(plan, e, raw):
    shape = jax.ShapeDtypeStruct((plan.rows, LANES), raw.dtype)
    hbm = pl.BlockSpec(memory_space=pltpu.HBM)
    return pl.pallas_call(
        functools.partial(prepare_kernel, plan, PREP_CHUNKS),
        out_shape=[jax.ShapeDtypeStruct((2, plan.rows, LANES), raw.dtype), shape, shape],
        in_specs=[hbm] * 2,
        out_specs=[vmem()] * 3,
        scratch_shapes=[
            pltpu.SMEM(e.shape, e.dtype),
            pltpu.VMEM(raw.shape, raw.dtype),
            pltpu.VMEM(raw.shape, jnp.float32),
            pltpu.SemaphoreType.DMA((PREP_CHUNKS + 1,)),
        ],
        compiler_params=pltpu.CompilerParams(vmem_limit_bytes=PREP_BYTES),
        cost_estimate=cost(10**6, 10**6),
        name="prepare",
    )(e, raw)


def make_tables(plan):
    g, m = plan.g, plan.modes
    shapes = (
        ((LANES, 2 * LANES), jnp.bfloat16),
        ((m, 3 * g), jnp.bfloat16),
        ((2 * g, 2 * m), jnp.bfloat16),
        ((2 * g, 2 * LANES), jnp.bfloat16),
        ((g, m, LANES), jnp.float32),
    )
    return pl.pallas_call(
        functools.partial(tables_kernel, plan),
        out_shape=[jax.ShapeDtypeStruct(*shape) for shape in shapes],
        out_specs=[vmem()] * len(shapes),
        compiler_params=params(),
        cost_estimate=cost(10**7, 10**6),
        name="tables",
    )()


def solve(plan, role, step, e, w, x, tables, extra=()):
    g, m = plan.g, plan.modes
    term = jax.ShapeDtypeStruct((plan.tiles, g, LANES), jnp.float32)
    out = {
        "visiting": term,
        "visiting_sum": jax.ShapeDtypeStruct((2,) + term.shape, term.dtype),
        "resident": term,
        "last": jax.ShapeDtypeStruct((2 * plan.rows, LANES), w.dtype),
    }[role]
    more = {"visiting_sum": [smem(), vmem()], "last": [vmem()] * 2}.get(role, [])
    return pl.pallas_call(
        functools.partial(solve_kernel, plan, role, step),
        out_shape=out,
        in_specs=[smem()] + [vmem()] * 7 + more,
        out_specs=vmem(),
        scratch_shapes=[
            pltpu.VMEM((plan.rows, LANES), jnp.float32),
            pltpu.VMEM((plan.rows + plan.pad, LANES), jnp.float32),
            pltpu.VMEM((plan.tiles, g, LANES), jnp.float32),
            pltpu.VMEM((g * g, LANES), jnp.bfloat16),
            pltpu.VMEM((g * g, LANES), jnp.bfloat16),
            pltpu.VMEM((g * g, LANES), jnp.bfloat16),
            pltpu.VMEM((g, m, LANES), jnp.float32),
            pltpu.VMEM((g * m, LANES), jnp.bfloat16),
            pltpu.VMEM((g * m, LANES), jnp.bfloat16),
            pltpu.VMEM((g * g, 2 * LANES), jnp.bfloat16),
        ]
        + ([pltpu.VMEM((2 * plan.rows, LANES), jnp.float32)] if role == "last" else []),
        compiler_params=params(),
        cost_estimate=cost(2 * 10**8, 4 * 10**6),
    )(e, w, x, *tables, *extra)


def per_device(wannier, pairs):
    plan = Plan(wannier.shape[1])
    count = lax.axis_size("blk")

    def shifted(array, by):
        return lax.ppermute(array, "blk", [(i, (i + by) % count) for i in range(count)])

    raw = wannier.reshape(2, plan.rows, LANES).transpose(1, 0, 2).reshape(2 * plan.rows, LANES)
    w, a1, a2 = prepare(plan, pairs, raw)
    e1 = shifted(pairs, -1)
    e2 = shifted(pairs, -2)
    a1 = shifted(a1, -1)
    a2 = shifted(a2, -2)
    b1 = pick(0, e1, w)
    b2 = pick(1, e2, w)
    b1 = shifted(b1, 1)
    b2 = shifted(b2, 2)
    tables = make_tables(plan)
    t1 = solve(plan, "visiting", 0, e1, w, a1, tables)
    partial = solve(plan, "visiting_sum", 1, e2, w, a2, tables, (e1, t1))
    r1 = solve(plan, "resident", 0, pairs, w, b1, tables)
    out = solve(plan, "last", 1, pairs, w, b2, tables, (partial, r1))
    out = out.reshape(plan.rows, 2, LANES).transpose(1, 0, 2)
    return out.reshape(wannier.shape)


def solution(mesh):
    return jax.shard_map(
        per_device,
        mesh=mesh,
        in_specs=(P("blk", None), P("blk", None, None, None)),
        out_specs=P("blk", None),
        check_vma=False,
    )
```

profile of v0, /device:TPU:0, one launch (start us, length us, event | category | flops | bytes accessed | tf_op | source)
XLA Modules:
  0.0 41.6 jit_solution(4137699217941656077)
XLA Ops:
  0.0 2.0 %prepare.1 = (bf16[2,864,128]{2,1,0:T(8,128)(2,1)}, bf16[864,128]{1,0:T(8,128)(2,1)}, bf16[864,128]{1,0:T(8,128)(2,1)}) custom-call(s32[1,2,1,6]{3,2,1,0:T(1,128)} %refs_0_.3, bf16[1728,128]{1,0:T(8,128)(2,1)} %bitcast.10), custom_call_target="tpu_custom_call" | custom-call | flops 1000000 | bytes 1000000 | tf_op jit(solution)/shard_map/prepare/pallas_call | solution.py:307
  2.0 6.5 %collective-permute-start.4 = (bf16[864,128]{1,0:T(8,128)(2,1)}, bf16[864,128]{1,0:T(8,128)(2,1)S(1)}, u32[]{:S(2)}, u32[]{:S(2)}) collective-permute-start(bf16[864,128]{1,0:T(8,128)(2,1)} %get-tuple-element.20), channel_id=1, source_target_pairs={{0,31},{1,0},{2,1},{3,2},{4,3},{5,4},{6,5},{7,6},{8,7},{9,8},{10,9... | collective-permute-start | bytes 663560 | tf_op jit(solution)/shard_map/ppermute | solution.py:381
  8.5 0.6 %collective-permute-start.2 = (bf16[864,128]{1,0:T(8,128)(2,1)}, bf16[864,128]{1,0:T(8,128)(2,1)S(1)}, u32[]{:S(2)}, u32[]{:S(2)}) collective-permute-start(bf16[864,128]{1,0:T(8,128)(2,1)} %get-tuple-element.19), channel_id=1, source_target_pairs={{0,30},{1,31},{2,0},{3,1},{4,2},{5,3},{6,4},{7,5},{8,6},{9,7},{10,... | collective-permute-start | bytes 663560 | tf_op jit(solution)/shard_map/ppermute | solution.py:381
  9.1 0.3 collective-permute-start.3
  9.4 7.6 %collective-permute-done.3.refs_0_.refs_8_.e_ref = s32[1,2,1,6]{3,2,1,0:T(1,128)S(1)} collective-permute-done((s32[1,2,1,6]{3,2,1,0:T(1,128)}, s32[1,2,1,6]{3,2,1,0:T(1,128)S(1)}, u32[]{:S(2)}, u32[]{:S(2)}) %collective-permute-start.3) | collective-permute-done | bytes 80 | tf_op jit(solution)/shard_map/ppermute | solution.py:381
  17.0 0.0 copy-start
  17.0 1.0 %copy-done = bf16[2,864,128]{2,1,0:T(8,128)(2,1)S(1)} copy-done((bf16[2,864,128]{2,1,0:T(8,128)(2,1)S(1)}, bf16[2,864,128]{2,1,0:T(8,128)(2,1)}, u32[]{:S(2)}) %copy-start) | copy-done | bytes 442392
  18.0 0.6 %pick.3 = bf16[864,128]{1,0:T(8,128)(2,1)S(1)} custom-call(s32[1,2,1,6]{3,2,1,0:T(1,128)S(1)} %collective-permute-done.3.refs_0_.refs_8_.e_ref, bf16[2,864,128]{2,1,0:T(8,128)(2,1)S(1)} %copy-done), custom_call_target="tpu_custom_call" | custom-call | flops 1000000 | bytes 1000000 | tf_op jit(solution)/shard_map/pick/pallas_call | solution.py:293
  18.6 0.1 collective-permute-start.5
  18.7 6.1 %collective-permute-start = (s32[1,2,1,6]{3,2,1,0:T(1,128)}, s32[1,2,1,6]{3,2,1,0:T(1,128)S(1)}, u32[]{:S(2)}, u32[]{:S(2)}) collective-permute-start(s32[1,2,1,6]{3,2,1,0:T(1,128)} %refs_0_.3), channel_id=1, source_target_pairs={{0,30},{1,31},{2,0},{3,1},{4,2},{5,3},{6,4},{7,5},{8,6},{9,7},{10,... | collective-permute-start | bytes 152 | tf_op jit(solution)/shard_map/ppermute | solution.py:381
  24.7 1.5 %collective-permute-done.e_ref.refs_0_ = s32[1,2,1,6]{3,2,1,0:T(1,128)S(1)} collective-permute-done((s32[1,2,1,6]{3,2,1,0:T(1,128)}, s32[1,2,1,6]{3,2,1,0:T(1,128)S(1)}, u32[]{:S(2)}, u32[]{:S(2)}) %collective-permute-start) | collective-permute-done | bytes 80 | tf_op jit(solution)/shard_map/ppermute | solution.py:381
  26.2 0.6 %pick.2 = bf16[864,128]{1,0:T(8,128)(2,1)S(1)} custom-call(s32[1,2,1,6]{3,2,1,0:T(1,128)S(1)} %collective-permute-done.e_ref.refs_0_, bf16[2,864,128]{2,1,0:T(8,128)(2,1)S(1)} %copy-done), custom_call_target="tpu_custom_call" | custom-call | flops 1000000 | bytes 1000000 | tf_op jit(solution)/shard_map/pick/pallas_call | solution.py:293
  26.8 0.1 collective-permute-start.1
  26.9 0.8 %tables.1 = (bf16[128,256]{1,0:T(8,128)(2,1)S(1)}, bf16[96,144]{1,0:T(8,128)(2,1)S(1)}, bf16[96,192]{1,0:T(8,128)(2,1)S(1)}, bf16[96,256]{1,0:T(8,128)(2,1)S(1)}, f32[48,96,128]{2,1,0:T(8,128)S(1)}) custom-call(), custom_call_target="tpu_custom_call" | custom-call | flops 10000000 | bytes 1000000 | tf_op jit(solution)/shard_map/tables/pallas_call | solution.py:333
  27.7 0.0 collective-permute-done.4.refs_2_
  27.7 0.0 copy-start.1
  27.7 1.0 %copy-done.1 = bf16[2,864,128]{2,1,0:T(8,128)(2,1)S(1)} copy-done((bf16[2,864,128]{2,1,0:T(8,128)(2,1)S(1)}, bf16[2,864,128]{2,1,0:T(8,128)(2,1)}, u32[]{:S(2)}) %copy-start.1) | copy-done | bytes 442392
  28.7 3.1 %shard_map.28.refs_9_ = f32[18,48,128]{2,1,0:T(8,128)S(1)} custom-call(s32[1,2,1,6]{3,2,1,0:T(1,128)S(1)} %collective-permute-done.3.refs_0_.refs_8_.e_ref, bf16[2,864,128]{2,1,0:T(8,128)(2,1)S(1)} %copy-done.1, bf16[864,128]{1,0:T(8,128)(2,1)S(1)} %collective-permute-done.4.refs_2_, bf16[128,256]{1,0:T(8,128)(2,1)S(1)} %get-tuple-element.14.refs_3_, ...), custom_call_target="tpu_custom_call" | custom-call | flops 200000000 | bytes 4000000 | tf_op jit(solution)/shard_map/pallas_call | solution.py:353
  31.8 0.0 copy-start.2
  31.8 0.0 copy-start.3
  31.9 0.0 collective-permute-done.2.refs_2_
  31.9 3.1 %shard_map.29.refs_8_ = f32[2,18,48,128]{3,2,1,0:T(8,128)S(1)} custom-call(s32[1,2,1,6]{3,2,1,0:T(1,128)S(1)} %collective-permute-done.e_ref.refs_0_, bf16[2,864,128]{2,1,0:T(8,128)(2,1)S(1)} %copy-done.1, bf16[864,128]{1,0:T(8,128)(2,1)S(1)} %collective-permute-done.2.refs_2_, bf16[128,256]{1,0:T(8,128)(2,1)S(1)} %get-tuple-element.14.refs_3_, ...), custom_call_target="tpu_custom_call" | custom-call | flops 200000000 | bytes 4000000 | tf_op jit(solution)/shard_map/pallas_call | solution.py:353
  35.0 0.0 collective-permute-done.5.refs_2_
  35.0 0.0 copy-done.2
  35.0 0.0 copy-done.3
  35.0 2.9 %shard_map.30.refs_9_ = f32[18,48,128]{2,1,0:T(8,128)S(1)} custom-call(s32[1,2,1,6]{3,2,1,0:T(1,128)S(1)} %copy-done.3, bf16[2,864,128]{2,1,0:T(8,128)(2,1)S(1)} %copy-done.2, bf16[864,128]{1,0:T(8,128)(2,1)S(1)} %collective-permute-done.5.refs_2_, bf16[128,256]{1,0:T(8,128)(2,1)S(1)} %get-tuple-element.14.refs_3_, ...), custom_call_target="tpu_custom_call" | custom-call | flops 200000000 | bytes 4000000 | tf_op jit(solution)/shard_map/pallas_call | solution.py:353
  37.9 0.0 collective-permute-done.1.refs_2_
  37.9 3.7 %shard_map.31 = bf16[1728,128]{1,0:T(8,128)(2,1)} custom-call(s32[1,2,1,6]{3,2,1,0:T(1,128)S(1)} %copy-done.3, bf16[2,864,128]{2,1,0:T(8,128)(2,1)S(1)} %copy-done.2, bf16[864,128]{1,0:T(8,128)(2,1)S(1)} %collective-permute-done.1.refs_2_, bf16[128,256]{1,0:T(8,128)(2,1)S(1)} %get-tuple-element.14.refs_3_, bf16[96,144]{1,0:T(8,128)(2,1)S(1)} %get-tuple-element.15.refs_4_, ...), custom_call_target="tpu_custom_call" | custom-call | flops 200000000 | bytes 4000000 | tf_op jit(solution)/shard_map/pallas_call | solution.py:353
Async XLA Ops:
  2.0 25.7 %collective-permute-start.4 = (bf16[864,128]{1,0:T(8,128)(2,1)}, bf16[864,128]{1,0:T(8,128)(2,1)S(1)}, u32[]{:S(2)}, u32[]{:S(2)}) collective-permute-start(bf16[864,128]{1,0:T(8,128)(2,1)} %get-tuple-element.20), channel_id=1, source_target_pairs={{0,31},{1,0},{2,1},{3,2},{4,3},{5,4},{6,5},{7,6},{8,7},{9,8},{10,9... | collective-permute-start | bytes 663560 | tf_op jit(solution)/shard_map/ppermute | solution.py:381
  8.5 23.4 %collective-permute-start.2 = (bf16[864,128]{1,0:T(8,128)(2,1)}, bf16[864,128]{1,0:T(8,128)(2,1)S(1)}, u32[]{:S(2)}, u32[]{:S(2)}) collective-permute-start(bf16[864,128]{1,0:T(8,128)(2,1)} %get-tuple-element.19), channel_id=1, source_target_pairs={{0,30},{1,31},{2,0},{3,1},{4,2},{5,3},{6,4},{7,5},{8,6},{9,7},{10,... | collective-permute-start | bytes 663560 | tf_op jit(solution)/shard_map/ppermute | solution.py:381
  9.1 7.9 %collective-permute-start.3 = (s32[1,2,1,6]{3,2,1,0:T(1,128)}, s32[1,2,1,6]{3,2,1,0:T(1,128)S(1)}, u32[]{:S(2)}, u32[]{:S(2)}) collective-permute-start(s32[1,2,1,6]{3,2,1,0:T(1,128)} %refs_0_.3), channel_id=1, source_target_pairs={{0,31},{1,0},{2,1},{3,2},{4,3},{5,4},{6,5},{7,6},{8,7},{9,8},{10,9... | collective-permute-start | bytes 152 | tf_op jit(solution)/shard_map/ppermute | solution.py:381
  17.0 1.0 %copy-start = (bf16[2,864,128]{2,1,0:T(8,128)(2,1)S(1)}, bf16[2,864,128]{2,1,0:T(8,128)(2,1)}, u32[]{:S(2)}) copy-start(bf16[2,864,128]{2,1,0:T(8,128)(2,1)} %get-tuple-element.13.w_ref.refs_1_) | copy-start | bytes 1327108
  18.6 16.4 %collective-permute-start.5 = (bf16[864,128]{1,0:T(8,128)(2,1)S(1)}, bf16[864,128]{1,0:T(8,128)(2,1)S(1)}, u32[]{:S(2)}, u32[]{:S(2)}) collective-permute-start(bf16[864,128]{1,0:T(8,128)(2,1)S(1)} %pick.3), channel_id=1, source_target_pairs={{0,1},{1,2},{2,3},{3,4},{4,5},{5,6},{6,7},{7,8},{8,9},{9,10},{10,1... | collective-permute-start | bytes 663560 | tf_op jit(solution)/shard_map/ppermute | solution.py:381
  18.7 7.6 %collective-permute-start = (s32[1,2,1,6]{3,2,1,0:T(1,128)}, s32[1,2,1,6]{3,2,1,0:T(1,128)S(1)}, u32[]{:S(2)}, u32[]{:S(2)}) collective-permute-start(s32[1,2,1,6]{3,2,1,0:T(1,128)} %refs_0_.3), channel_id=1, source_target_pairs={{0,30},{1,31},{2,0},{3,1},{4,2},{5,3},{6,4},{7,5},{8,6},{9,7},{10,... | collective-permute-start | bytes 152 | tf_op jit(solution)/shard_map/ppermute | solution.py:381
  26.8 11.1 %collective-permute-start.1 = (bf16[864,128]{1,0:T(8,128)(2,1)S(1)}, bf16[864,128]{1,0:T(8,128)(2,1)S(1)}, u32[]{:S(2)}, u32[]{:S(2)}) collective-permute-start(bf16[864,128]{1,0:T(8,128)(2,1)S(1)} %pick.2), channel_id=1, source_target_pairs={{0,2},{1,3},{2,4},{3,5},{4,6},{5,7},{6,8},{7,9},{8,10},{9,11},{10,... | collective-permute-start | bytes 663560 | tf_op jit(solution)/shard_map/ppermute | solution.py:381
  27.7 1.0 %copy-start.1 = (bf16[2,864,128]{2,1,0:T(8,128)(2,1)S(1)}, bf16[2,864,128]{2,1,0:T(8,128)(2,1)}, u32[]{:S(2)}) copy-start(bf16[2,864,128]{2,1,0:T(8,128)(2,1)} %get-tuple-element.13.w_ref.refs_1_) | copy-start | bytes 1327108
  31.8 3.2 %copy-start.2 = (bf16[2,864,128]{2,1,0:T(8,128)(2,1)S(1)}, bf16[2,864,128]{2,1,0:T(8,128)(2,1)}, u32[]{:S(2)}) copy-start(bf16[2,864,128]{2,1,0:T(8,128)(2,1)} %get-tuple-element.13.w_ref.refs_1_) | copy-start | bytes 1327108
  31.8 3.2 %copy-start.3 = (s32[1,2,1,6]{3,2,1,0:T(1,128)S(1)}, s32[1,2,1,6]{3,2,1,0:T(1,128)}, u32[]{:S(2)}) copy-start(s32[1,2,1,6]{3,2,1,0:T(1,128)} %refs_0_.3) | copy-start | bytes 148
where the time goes:
time: 42.2 us; the launch traced here: 41.6 us
  Pallas kernels  16.8 us (40%)
  starting transfers between devices  13.6 us (32%)
  waiting for transfers between devices  9.1 us (22%)
  local copies, waits for them, and re-layouts  2.03 us (5%)
    ppermute x6, starting transfers between devices, shifted(): lax.ppermute(array, 'blk', [(i, (i + by) % count) for i in range(count)])  13.6 us
    pallas_call x4, Pallas kernels, solve(): pl.pallas_call(functools.partial(solve_kernel, plan, role, step), out_sha...  12.8 us
    ppermute x6, waiting for transfers between devices, shifted(): lax.ppermute(array, 'blk', [(i, (i + by) % count) for i in range(count)])  9.1 us
    pallas_call x1, Pallas kernels, prepare(): pl.pallas_call(functools.partial(prepare_kernel, plan, PREP_CHUNKS), out_...  2.03 us
    unnamed x8, local copies, waits for them, and re-layouts  2.03 us
    pallas_call x2, Pallas kernels, pick(): pl.pallas_call(functools.partial(pick_kernel, step), out_shape=jax.ShapeD...  1.13 us
  transfers between devices with their start and end apart: 6, of which 2 were waited for; matrix products, arithmetic and copies ran while one was open for 0% of the time, Pallas kernels for 27%

commit v1 on v0

--- a/solution.py
+++ b/solution.py
@@ -11,7 +11,7 @@
 
 LANES = 128
 VMEM_BYTES = 20 * 1024 * 1024
-PREP_BYTES = 64380928
+PREP_BYTES = 20963328
 PREP_CHUNKS = 4
 
 
@@ -92,8 +92,8 @@
     for copy in copies[-1:] + copies[:-1]:
         copy.start()
     copies[-1].wait()
-    first = e_ref[0, 0, 0, 0] == 0
-    second = e_ref[0, 1, 0, 0] == 0
+    entries = e_ref[0, 0], e_ref[0, 1]
+    first, second = [entry[0, 0] == 0 for entry in entries]
     for at in range(chunks):
         copies[at].wait()
         here = pl.ds(rows * at, rows)
@@ -106,7 +106,8 @@
 
 
 def pick_kernel(step, e_ref, w_ref, out_ref):
-    out_ref[...] = w_ref[e_ref[0, step, 0, 1]]
+    entry = e_ref[0, step]
+    out_ref[...] = w_ref[entry[0, 1]]
 
 
 def solve_kernel(plan, role, step, *refs):
@@ -115,17 +116,16 @@
     refs = refs[8:]
     if role == "visiting_sum":
         (other_e_ref, other_ref), refs = refs[:2], refs[2:]
+        other_entry = other_e_ref[0, 0]
     if role == "last":
         (partial_ref, other_ref), refs = refs[:2], refs[2:]
+        other_entry = e_ref[0, 0]
     out_ref, a_pad, b_pad, b_sh, rho_t, x_hi, x_lo, z, y_hi, y_lo, v = refs[:11]
     both = refs[11] if role == "last" else None
     g, m = plan.g, plan.modes
-    r_at = e_ref[0, step, 0, 0]
-    v_at = e_ref[0, step, 0, 1]
-    ox = e_ref[0, step, 0, 2]
-    oy = e_ref[0, step, 0, 3]
-    oz = e_ref[0, step, 0, 4]
-    live = e_ref[0, step, 0, 5].astype(jnp.float32)
+    entry = e_ref[0, step]
+    r_at, v_at, ox, oy, oz, live = [entry[0, at] for at in range(6)]
+    live = live.astype(jnp.float32)
     shift = ox * (g * g) + oy * g + oz
     down = lax.shift_right_logical(shift, 7)
     roll = shift & (LANES - 1)
@@ -229,7 +229,7 @@
                     out_ref[t] = phi * b_sh[t]
                 else:
                     own, other = phi * b_sh[t], other_ref[t]
-                    other_at = e_ref[0, 0, 0, 0]
+                    other_at = other_entry[0, 0]
                     for f in range(2):
                         total = partial_ref[f, t]
                         total = total + jnp.where(other_at == f, other, 0.0) + jnp.where(r_at == f, own, 0.0)
@@ -266,17 +266,13 @@
             if role == "visiting":
                 out_ref[t] = term
                 continue
-            other, other_at = other_ref[t], other_e_ref[0, 0, 0, 1]
+            other, other_at = other_ref[t], other_entry[0, 1]
             for f in range(2):
                 out_ref[f, t] = jnp.where(other_at == f, other, 0.0) + jnp.where(v_at == f, term, 0.0)
     if role == "last":
         out_ref[...] = both[...].astype(jnp.bfloat16)
 
 
-def smem():
-    return pl.BlockSpec(memory_space=pltpu.SMEM)
-
-
 def vmem():
     return pl.BlockSpec(memory_space=pltpu.VMEM)
 
@@ -293,7 +289,7 @@
     return pl.pallas_call(
         functools.partial(pick_kernel, step),
         out_shape=jax.ShapeDtypeStruct(w.shape[1:], w.dtype),
-        in_specs=[smem(), vmem()],
+        in_specs=[vmem(), vmem()],
         out_specs=vmem(),
         compiler_params=params(),
         cost_estimate=cost(10**6, 10**6),
@@ -306,11 +302,15 @@
     hbm = pl.BlockSpec(memory_space=pltpu.HBM)
     return pl.pallas_call(
         functools.partial(prepare_kernel, plan, PREP_CHUNKS),
-        out_shape=[jax.ShapeDtypeStruct((2, plan.rows, LANES), raw.dtype), shape, shape],
+        out_shape=[
+            jax.ShapeDtypeStruct((2, plan.rows, LANES), raw.dtype),
+            shape,
+            shape,
+            jax.ShapeDtypeStruct(e.shape, e.dtype),
+        ],
         in_specs=[hbm] * 2,
-        out_specs=[vmem()] * 3,
+        out_specs=[vmem()] * 4,
         scratch_shapes=[
-            pltpu.SMEM(e.shape, e.dtype),
             pltpu.VMEM(raw.shape, raw.dtype),
             pltpu.VMEM(raw.shape, jnp.float32),
             pltpu.SemaphoreType.DMA((PREP_CHUNKS + 1,)),
@@ -349,11 +349,11 @@
         "resident": term,
         "last": jax.ShapeDtypeStruct((2 * plan.rows, LANES), w.dtype),
     }[role]
-    more = {"visiting_sum": [smem(), vmem()], "last": [vmem()] * 2}.get(role, [])
+    more = {"visiting_sum": [vmem()] * 2, "last": [vmem()] * 2}.get(role, [])
     return pl.pallas_call(
         functools.partial(solve_kernel, plan, role, step),
         out_shape=out,
-        in_specs=[smem()] + [vmem()] * 7 + more,
+        in_specs=[vmem()] * 8 + more,
         out_specs=vmem(),
         scratch_shapes=[
             pltpu.VMEM((plan.rows, LANES), jnp.float32),
@@ -381,7 +381,7 @@
         return lax.ppermute(array, "blk", [(i, (i + by) % count) for i in range(count)])
 
     raw = wannier.reshape(2, plan.rows, LANES).transpose(1, 0, 2).reshape(2 * plan.rows, LANES)
-    w, a1, a2 = prepare(plan, pairs, raw)
+    w, a1, a2, own = prepare(plan, pairs, raw)
     e1 = shifted(pairs, -1)
     e2 = shifted(pairs, -2)
     a1 = shifted(a1, -1)
@@ -393,8 +393,8 @@
     tables = make_tables(plan)
     t1 = solve(plan, "visiting", 0, e1, w, a1, tables)
     partial = solve(plan, "visiting_sum", 1, e2, w, a2, tables, (e1, t1))
-    r1 = solve(plan, "resident", 0, pairs, w, b1, tables)
-    out = solve(plan, "last", 1, pairs, w, b2, tables, (partial, r1))
+    r1 = solve(plan, "resident", 0, own, w, b1, tables)
+    out = solve(plan, "last", 1, own, w, b2, tables, (partial, r1))
     out = out.reshape(plan.rows, 2, LANES).transpose(1, 0, 2)
     return out.reshape(wannier.shape)
 

time: 42.2 us -> 39.1 us (0.927)
  Pallas kernels: 16.8 us -> 13 us
  waiting for transfers between devices: 9.1 us -> 10.5 us
    pallas_call x4, Pallas kernels: 12.8 us -> 11.1 us  [solve(): pl.pallas_call(functools.partial(solve_kernel, plan, role, step), out_sha...]
    ppermute x6, waiting for transfers between devices: 9.1 us -> 10.5 us  [shifted(): lax.ppermute(array, 'blk', [(i, (i + by) % count) for i in range(count)])]
    pallas_call x1, Pallas kernels: 2.03 us -> 0.82 us  [prepare(): pl.pallas_call(functools.partial(prepare_kernel, plan, PREP_CHUNKS), out_...]
    pallas_call x2, Pallas kernels: 1.13 us -> 0.24 us  [pick(): pl.pallas_call(functools.partial(pick_kernel, step), out_shape=jax.ShapeD...]
    unnamed x8 -> x4, local copies, waits for them, and re-layouts: 2.03 us -> 1.69 us
  transfers between devices with their start and end apart: 6 -> 6, of which waited for: 2 -> 3; matrix products, arithmetic and copies ran while one was open for 0% -> 0% of each run, Pallas kernels for 27% -> 23%
where the time goes in v1:
time: 39.1 us; the launch traced here: 38.9 us
  starting transfers between devices  13.7 us (35%)
  Pallas kernels  13 us (33%)
  waiting for transfers between devices  10.5 us (27%)
  local copies, waits for them, and re-layouts  1.69 us (4%)
    ppermute x6, starting transfers between devices, shifted(): lax.ppermute(array, 'blk', [(i, (i + by) % count) for i in range(count)])  13.7 us
    pallas_call x4, Pallas kernels, solve(): pl.pallas_call(functools.partial(solve_kernel, plan, role, step), out_sha...  11.1 us
    ppermute x6, waiting for transfers between devices, shifted(): lax.ppermute(array, 'blk', [(i, (i + by) % count) for i in range(count)])  10.5 us
    unnamed x4, local copies, waits for them, and re-layouts  1.69 us
    pallas_call x1, Pallas kernels, make_tables(): pl.pallas_call(functools.partial(tables_kernel, plan), out_shape=[jax.Sha...  0.83 us
    pallas_call x1, Pallas kernels, prepare(): pl.pallas_call(functools.partial(prepare_kernel, plan, PREP_CHUNKS), out_...  0.82 us
  transfers between devices with their start and end apart: 6, of which 3 were waited for; matrix products, arithmetic and copies ran while one was open for 0% of the time, Pallas kernels for 23%

profile of v1, /device:TPU:0, one launch (start us, length us, event | category | flops | bytes accessed | tf_op | source)
XLA Modules:
  0.0 38.9 jit_solution(1795744218792744259)
XLA Ops:
  0.0 0.0 copy-start
  0.0 1.0 %copy-done = bf16[2,110592]{1,0:T(2,128)(2,1)S(1)} copy-done((bf16[2,110592]{1,0:T(2,128)(2,1)S(1)}, bf16[2,110592]{1,0:T(2,128)(2,1)}, u32[]{:S(2)}) %copy-start) | copy-done | bytes 442392
  1.0 0.0 copy-start.1
  1.0 0.7 %copy-done.1 = s32[1,2,1,6]{3,2,1,0:T(1,128)S(1)} copy-done((s32[1,2,1,6]{3,2,1,0:T(1,128)S(1)}, s32[1,2,1,6]{3,2,1,0:T(1,128)}, u32[]{:S(2)}) %copy-start.1) | copy-done | bytes 72
  1.7 0.8 %prepare.1 = (bf16[2,864,128]{2,1,0:T(8,128)(2,1)S(1)}, bf16[864,128]{1,0:T(8,128)(2,1)S(1)}, bf16[864,128]{1,0:T(8,128)(2,1)S(1)}, s32[1,2,1,6]{3,2,1,0:T(1,128)S(1)}) custom-call(s32[1,2,1,6]{3,2,1,0:T(1,128)S(1)} %copy-done.1, bf16[1728,128]{1,0:T(8,128)(2,1)S(1)} %bitcast.10), custom_call_target="tpu_custom_call" | custom-call | flops 1000000 | bytes 1000000 | tf_op jit(solution)/shard_map/prepare/pallas_call | solution.py:303
  2.5 6.5 %collective-permute-start.4 = (bf16[864,128]{1,0:T(8,128)(2,1)S(1)}, bf16[864,128]{1,0:T(8,128)(2,1)S(1)}, u32[]{:S(2)}, u32[]{:S(2)}) collective-permute-start(bf16[864,128]{1,0:T(8,128)(2,1)S(1)} %get-tuple-element.22), channel_id=1, source_target_pairs={{0,31},{1,0},{2,1},{3,2},{4,3},{5,4},{6,5},{7,6},{8,7},{9,8},{10,9... | collective-permute-start | bytes 663560 | tf_op jit(solution)/shard_map/ppermute | solution.py:381
  9.0 0.6 %collective-permute-start.2 = (bf16[864,128]{1,0:T(8,128)(2,1)S(1)}, bf16[864,128]{1,0:T(8,128)(2,1)S(1)}, u32[]{:S(2)}, u32[]{:S(2)}) collective-permute-start(bf16[864,128]{1,0:T(8,128)(2,1)S(1)} %get-tuple-element.21), channel_id=1, source_target_pairs={{0,30},{1,31},{2,0},{3,1},{4,2},{5,3},{6,4},{7,5},{8,6},{9,7},{10,... | collective-permute-start | bytes 663560 | tf_op jit(solution)/shard_map/ppermute | solution.py:381
  9.6 0.3 collective-permute-start.3
  9.9 7.3 %collective-permute-done.3.refs_0_.refs_8_.e_ref = s32[1,2,1,6]{3,2,1,0:T(1,128)S(1)} collective-permute-done((s32[1,2,1,6]{3,2,1,0:T(1,128)S(1)}, s32[1,2,1,6]{3,2,1,0:T(1,128)S(1)}, u32[]{:S(2)}, u32[]{:S(2)}) %collective-permute-start.3) | collective-permute-done | bytes 80 | tf_op jit(solution)/shard_map/ppermute | solution.py:381
  17.2 0.1 pick.3
  17.3 0.1 collective-permute-start.5
  17.4 6.2 %collective-permute-start = (s32[1,2,1,6]{3,2,1,0:T(1,128)}, s32[1,2,1,6]{3,2,1,0:T(1,128)S(1)}, u32[]{:S(2)}, u32[]{:S(2)}) collective-permute-start(s32[1,2,1,6]{3,2,1,0:T(1,128)} %e_hbm.1), channel_id=1, source_target_pairs={{0,30},{1,31},{2,0},{3,1},{4,2},{5,3},{6,4},{7,5},{8,6},{9,7},{10,... | collective-permute-start | bytes 152 | tf_op jit(solution)/shard_map/ppermute | solution.py:381
  23.5 1.5 %collective-permute-done.e_ref.refs_0_ = s32[1,2,1,6]{3,2,1,0:T(1,128)S(1)} collective-permute-done((s32[1,2,1,6]{3,2,1,0:T(1,128)}, s32[1,2,1,6]{3,2,1,0:T(1,128)S(1)}, u32[]{:S(2)}, u32[]{:S(2)}) %collective-permute-start) | collective-permute-done | bytes 80 | tf_op jit(solution)/shard_map/ppermute | solution.py:381
  25.0 0.1 pick.2
  25.2 0.1 collective-permute-start.1
  25.2 0.8 %tables.1 = (bf16[128,256]{1,0:T(8,128)(2,1)S(1)}, bf16[96,144]{1,0:T(8,128)(2,1)S(1)}, bf16[96,192]{1,0:T(8,128)(2,1)S(1)}, bf16[96,256]{1,0:T(8,128)(2,1)S(1)}, f32[48,96,128]{2,1,0:T(8,128)S(1)}) custom-call(), custom_call_target="tpu_custom_call" | custom-call | flops 10000000 | bytes 1000000 | tf_op jit(solution)/shard_map/tables/pallas_call | solution.py:333
  26.1 0.0 collective-permute-done.4.refs_2_
  26.1 2.6 %shard_map.28.refs_9_ = f32[18,48,128]{2,1,0:T(8,128)S(1)} custom-call(s32[1,2,1,6]{3,2,1,0:T(1,128)S(1)} %collective-permute-done.3.refs_0_.refs_8_.e_ref, bf16[2,864,128]{2,1,0:T(8,128)(2,1)S(1)} %get-tuple-element.15.w_ref.refs_1_, bf16[864,128]{1,0:T(8,128)(2,1)S(1)} %collective-permute-done.4.refs_2_, bf16[128,256]{1,0:T(8,128)(2,1)S(1)} %get-tuple-element.16.refs_3_, ...), custom_call_target="tpu_custom_call" | custom-call | flops 200000000 | bytes 4000000 | tf_op jit(solution)/shard_map/pallas_call | solution.py:353
  28.7 0.0 collective-permute-done.2.refs_2_
  28.7 2.6 %shard_map.29.refs_8_ = f32[2,18,48,128]{3,2,1,0:T(8,128)S(1)} custom-call(s32[1,2,1,6]{3,2,1,0:T(1,128)S(1)} %collective-permute-done.e_ref.refs_0_, bf16[2,864,128]{2,1,0:T(8,128)(2,1)S(1)} %get-tuple-element.15.w_ref.refs_1_, bf16[864,128]{1,0:T(8,128)(2,1)S(1)} %collective-permute-done.2.refs_2_, bf16[128,256]{1,0:T(8,128)(2,1)S(1)} %get-tuple-element.16.refs_3_, ...), custom_call_target="tpu_custom_call" | custom-call | flops 200000000 | bytes 4000000 | tf_op jit(solution)/shard_map/pallas_call | solution.py:353
  31.4 0.0 collective-permute-done.5.refs_2_
  31.4 2.5 %shard_map.30.refs_9_ = f32[18,48,128]{2,1,0:T(8,128)S(1)} custom-call(s32[1,2,1,6]{3,2,1,0:T(1,128)S(1)} %get-tuple-element.14.refs_0_, bf16[2,864,128]{2,1,0:T(8,128)(2,1)S(1)} %get-tuple-element.15.w_ref.refs_1_, bf16[864,128]{1,0:T(8,128)(2,1)S(1)} %collective-permute-done.5.refs_2_, bf16[128,256]{1,0:T(8,128)(2,1)S(1)} %get-tuple-element.16.refs_3_, ...), custom_call_target="tpu_custom_call" | custom-call | flops 200000000 | bytes 4000000 | tf_op jit(solution)/shard_map/pallas_call | solution.py:353
  33.9 1.7 %collective-permute-done.1.refs_2_ = bf16[864,128]{1,0:T(8,128)(2,1)S(1)} collective-permute-done((bf16[864,128]{1,0:T(8,128)(2,1)S(1)}, bf16[864,128]{1,0:T(8,128)(2,1)S(1)}, u32[]{:S(2)}, u32[]{:S(2)}) %collective-permute-start.1) | collective-permute-done | bytes 221216 | tf_op jit(solution)/shard_map/ppermute | solution.py:381
  35.6 3.3 %shard_map.31 = bf16[1728,128]{1,0:T(8,128)(2,1)} custom-call(s32[1,2,1,6]{3,2,1,0:T(1,128)S(1)} %get-tuple-element.14.refs_0_, bf16[2,864,128]{2,1,0:T(8,128)(2,1)S(1)} %get-tuple-element.15.w_ref.refs_1_, bf16[864,128]{1,0:T(8,128)(2,1)S(1)} %collective-permute-done.1.refs_2_, bf16[128,256]{1,0:T(8,128)(2,1)S(1)} %get-tuple-element.16.refs_3_, ...), custom_call_target="tpu_custom_call" | custom-call | flops 200000000 | bytes 4000000 | tf_op jit(solution)/shard_map/pallas_call | solution.py:353
Async XLA Ops:
  0.0 1.0 %copy-start = (bf16[2,110592]{1,0:T(2,128)(2,1)S(1)}, bf16[2,110592]{1,0:T(2,128)(2,1)}, u32[]{:S(2)}) copy-start(bf16[2,110592]{1,0:T(2,128)(2,1)} %param.2) | copy-start | bytes 1327108
  1.0 0.7 %copy-start.1 = (s32[1,2,1,6]{3,2,1,0:T(1,128)S(1)}, s32[1,2,1,6]{3,2,1,0:T(1,128)}, u32[]{:S(2)}) copy-start(s32[1,2,1,6]{3,2,1,0:T(1,128)} %e_hbm.1) | copy-start | bytes 148
  2.5 23.6 %collective-permute-start.4 = (bf16[864,128]{1,0:T(8,128)(2,1)S(1)}, bf16[864,128]{1,0:T(8,128)(2,1)S(1)}, u32[]{:S(2)}, u32[]{:S(2)}) collective-permute-start(bf16[864,128]{1,0:T(8,128)(2,1)S(1)} %get-tuple-element.22), channel_id=1, source_target_pairs={{0,31},{1,0},{2,1},{3,2},{4,3},{5,4},{6,5},{7,6},{8,7},{9,8},{10,9... | collective-permute-start | bytes 663560 | tf_op jit(solution)/shard_map/ppermute | solution.py:381
  9.0 19.8 %collective-permute-start.2 = (bf16[864,128]{1,0:T(8,128)(2,1)S(1)}, bf16[864,128]{1,0:T(8,128)(2,1)S(1)}, u32[]{:S(2)}, u32[]{:S(2)}) collective-permute-start(bf16[864,128]{1,0:T(8,128)(2,1)S(1)} %get-tuple-element.21), channel_id=1, source_target_pairs={{0,30},{1,31},{2,0},{3,1},{4,2},{5,3},{6,4},{7,5},{8,6},{9,7},{10,... | collective-permute-start | bytes 663560 | tf_op jit(solution)/shard_map/ppermute | solution.py:381
  9.6 7.6 %collective-permute-start.3 = (s32[1,2,1,6]{3,2,1,0:T(1,128)S(1)}, s32[1,2,1,6]{3,2,1,0:T(1,128)S(1)}, u32[]{:S(2)}, u32[]{:S(2)}) collective-permute-start(s32[1,2,1,6]{3,2,1,0:T(1,128)S(1)} %copy-done.1), channel_id=1, source_target_pairs={{0,31},{1,0},{2,1},{3,2},{4,3},{5,4},{6,5},{7,6},{8,7},{9,8},{10,9... | collective-permute-start | bytes 152 | tf_op jit(solution)/shard_map/ppermute | solution.py:381
  17.3 14.1 %collective-permute-start.5 = (bf16[864,128]{1,0:T(8,128)(2,1)S(1)}, bf16[864,128]{1,0:T(8,128)(2,1)S(1)}, u32[]{:S(2)}, u32[]{:S(2)}) collective-permute-start(bf16[864,128]{1,0:T(8,128)(2,1)S(1)} %pick.3), channel_id=1, source_target_pairs={{0,1},{1,2},{2,3},{3,4},{4,5},{5,6},{6,7},{7,8},{8,9},{9,10},{10,1... | collective-permute-start | bytes 663560 | tf_op jit(solution)/shard_map/ppermute | solution.py:381
  17.4 7.7 %collective-permute-start = (s32[1,2,1,6]{3,2,1,0:T(1,128)}, s32[1,2,1,6]{3,2,1,0:T(1,128)S(1)}, u32[]{:S(2)}, u32[]{:S(2)}) collective-permute-start(s32[1,2,1,6]{3,2,1,0:T(1,128)} %e_hbm.1), channel_id=1, source_target_pairs={{0,30},{1,31},{2,0},{3,1},{4,2},{5,3},{6,4},{7,5},{8,6},{9,7},{10,... | collective-permute-start | bytes 152 | tf_op jit(solution)/shard_map/ppermute | solution.py:381
  25.2 10.4 %collective-permute-start.1 = (bf16[864,128]{1,0:T(8,128)(2,1)S(1)}, bf16[864,128]{1,0:T(8,128)(2,1)S(1)}, u32[]{:S(2)}, u32[]{:S(2)}) collective-permute-start(bf16[864,128]{1,0:T(8,128)(2,1)S(1)} %pick.2), channel_id=1, source_target_pairs={{0,2},{1,3},{2,4},{3,5},{4,6},{5,7},{6,8},{7,9},{8,10},{9,11},{10,... | collective-permute-start | bytes 663560 | tf_op jit(solution)/shard_map/ppermute | solution.py:381

commit v2 on v1

--- a/solution.py
+++ b/solution.py
@@ -13,6 +13,8 @@
 VMEM_BYTES = 20 * 1024 * 1024
 PREP_BYTES = 20963328
 PREP_CHUNKS = 4
+LAST_BYTES = 32 * 1024 * 1024
+LEAD = 3
 
 
 class Plan:
@@ -110,7 +112,7 @@
     out_ref[...] = w_ref[entry[0, 1]]
 
 
-def solve_kernel(plan, role, step, *refs):
+def solve_steps(plan, role, step, *refs):
     owner = role.startswith("visiting")
     (e_ref, w_ref, x_ref, start_ref, first_ref, last_ref, end_ref, ratio_ref) = refs[:8]
     refs = refs[8:]
@@ -242,6 +244,7 @@
             first(at - 1)
         if 0 <= at - 2 < parts:
             sweep_up(at - 2)
+        yield
     swept[0] = jnp.zeros((m, LANES), jnp.float32)
     if owner:
         b_pad[plan.rows :, :] = jnp.zeros((plan.pad, LANES), jnp.float32)
@@ -252,6 +255,7 @@
             last(parts - at)
         if 0 <= at - 2 < parts:
             end(parts + 1 - at)
+        yield
 
     if owner:
         back = (LANES - roll) & (LANES - 1)
@@ -271,6 +275,25 @@
                 out_ref[f, t] = jnp.where(other_at == f, other, 0.0) + jnp.where(v_at == f, term, 0.0)
     if role == "last":
         out_ref[...] = both[...].astype(jnp.bfloat16)
+
+
+def solve_kernel(plan, role, step, *refs):
+    for _ in solve_steps(plan, role, step, *refs):
+        pass
+
+
+def middle_kernel(plan, e2_ref, e1_ref, own_ref, w_ref, x1_ref, x2_ref, *refs):
+    tables, (t1_ref, partial_ref, term_ref), refs = refs[:5], refs[5:8], refs[8:]
+    early = solve_steps(
+        plan, "visiting_sum", 1, e2_ref, w_ref, x1_ref, *tables, e1_ref, t1_ref, partial_ref, *refs[:10]
+    )
+    late = solve_steps(plan, "resident", 0, own_ref, w_ref, x2_ref, *tables, term_ref, *refs[10:])
+    for _ in range(LEAD):
+        next(early)
+    for _ in early:
+        next(late)
+    for _ in late:
+        pass
 
 
 def vmem():
@@ -340,8 +363,38 @@
     )()
 
 
+def solve_scratch(plan):
+    g, m = plan.g, plan.modes
+    return [
+        pltpu.VMEM((plan.rows, LANES), jnp.float32),
+        pltpu.VMEM((plan.rows + plan.pad, LANES), jnp.float32),
+        pltpu.VMEM((plan.tiles, g, LANES), jnp.float32),
+        pltpu.VMEM((g * g, LANES), jnp.bfloat16),
+        pltpu.VMEM((g * g, LANES), jnp.bfloat16),
+        pltpu.VMEM((g * g, LANES), jnp.bfloat16),
+        pltpu.VMEM((g, m, LANES), jnp.float32),
+        pltpu.VMEM((g * m, LANES), jnp.bfloat16),
+        pltpu.VMEM((g * m, LANES), jnp.bfloat16),
+        pltpu.VMEM((g * g, 2 * LANES), jnp.bfloat16),
+    ]
+
+
+def solve_middle(plan, e2, e1, own, w, x1, x2, tables, t1):
+    term = jax.ShapeDtypeStruct((plan.tiles, plan.g, LANES), jnp.float32)
+    return pl.pallas_call(
+        functools.partial(middle_kernel, plan),
+        out_shape=[jax.ShapeDtypeStruct((2,) + term.shape, term.dtype), term],
+        in_specs=[vmem()] * 12,
+        out_specs=[vmem()] * 2,
+        scratch_shapes=solve_scratch(plan) * 2,
+        compiler_params=pltpu.CompilerParams(vmem_limit_bytes=LAST_BYTES),
+        cost_estimate=cost(4 * 10**8, 8 * 10**6),
+        name="solve_middle",
+    )(e2, e1, own, w, x1, x2, *tables, t1)
+
+
 def solve(plan, role, step, e, w, x, tables, extra=()):
-    g, m = plan.g, plan.modes
+    g = plan.g
     term = jax.ShapeDtypeStruct((plan.tiles, g, LANES), jnp.float32)
     out = {
         "visiting": term,
@@ -355,18 +408,7 @@
         out_shape=out,
         in_specs=[vmem()] * 8 + more,
         out_specs=vmem(),
-        scratch_shapes=[
-            pltpu.VMEM((plan.rows, LANES), jnp.float32),
-            pltpu.VMEM((plan.rows + plan.pad, LANES), jnp.float32),
-            pltpu.VMEM((plan.tiles, g, LANES), jnp.float32),
-            pltpu.VMEM((g * g, LANES), jnp.bfloat16),
-            pltpu.VMEM((g * g, LANES), jnp.bfloat16),
-            pltpu.VMEM((g * g, LANES), jnp.bfloat16),
-            pltpu.VMEM((g, m, LANES), jnp.float32),
-            pltpu.VMEM((g * m, LANES), jnp.bfloat16),
-            pltpu.VMEM((g * m, LANES), jnp.bfloat16),
-            pltpu.VMEM((g * g, 2 * LANES), jnp.bfloat16),
-        ]
+        scratch_shapes=solve_scratch(plan)
         + ([pltpu.VMEM((2 * plan.rows, LANES), jnp.float32)] if role == "last" else []),
         compiler_params=params(),
         cost_estimate=cost(2 * 10**8, 4 * 10**6),
@@ -392,8 +434,7 @@
     b2 = shifted(b2, 2)
     tables = make_tables(plan)
     t1 = solve(plan, "visiting", 0, e1, w, a1, tables)
-    partial = solve(plan, "visiting_sum", 1, e2, w, a2, tables, (e1, t1))
-    r1 = solve(plan, "resident", 0, own, w, b1, tables)
+    partial, r1 = solve_middle(plan, e2, e1, own, w, a2, b1, tables, t1)
     out = solve(plan, "last", 1, own, w, b2, tables, (partial, r1))
     out = out.reshape(plan.rows, 2, LANES).transpose(1, 0, 2)
     return out.reshape(wannier.shape)

time: 39.1 us -> 36.2 us (0.926)
  waiting for transfers between devices: 10.5 us -> 8.2 us
  Pallas kernels: 13 us -> 12.3 us
    pallas_call x4 -> x2, Pallas kernels: 11.1 us -> 5.96 us  [solve(): pl.pallas_call(functools.partial(solve_kernel, plan, role, step), out_sha...]
    pallas_call x0 -> x1, Pallas kernels: none -> 4.42 us  [solve_middle(): pl.pallas_call(functools.partial(middle_kernel, plan), out_shape=[jax.Sha...]
    ppermute x6, waiting for transfers between devices: 10.5 us -> 8.2 us  [shifted(): lax.ppermute(array, 'blk', [(i, (i + by) % count) for i in range(count)])]
where the time goes in v2:
time: 36.2 us; the launch traced here: 36 us
  starting transfers between devices  13.8 us (38%)
  Pallas kernels  12.3 us (34%)
  waiting for transfers between devices  8.2 us (23%)
  local copies, waits for them, and re-layouts  1.69 us (5%)
    ppermute x6, starting transfers between devices, shifted(): lax.ppermute(array, 'blk', [(i, (i + by) % count) for i in range(count)])  13.8 us
    ppermute x6, waiting for transfers between devices, shifted(): lax.ppermute(array, 'blk', [(i, (i + by) % count) for i in range(count)])  8.2 us
    pallas_call x2, Pallas kernels, solve(): pl.pallas_call(functools.partial(solve_kernel, plan, role, step), out_sha...  5.96 us
    pallas_call x1, Pallas kernels, solve_middle(): pl.pallas_call(functools.partial(middle_kernel, plan), out_shape=[jax.Sha...  4.42 us
    unnamed x4, local copies, waits for them, and re-layouts  1.69 us
    pallas_call x1, Pallas kernels, make_tables(): pl.pallas_call(functools.partial(tables_kernel, plan), out_shape=[jax.Sha...  0.83 us
    pallas_call x1, Pallas kernels, prepare(): pl.pallas_call(functools.partial(prepare_kernel, plan, PREP_CHUNKS), out_...  0.82 us
  transfers between devices with their start and end apart: 6, of which 3 were waited for; matrix products, arithmetic and copies ran while one was open for 0% of the time, Pallas kernels for 23%

profile of v2, /device:TPU:0, one launch (start us, length us, event | category | flops | bytes accessed | tf_op | source)
XLA Modules:
  0.0 36.0 jit_solution(16431538175564264220)
XLA Ops:
  0.0 0.0 copy-start
  0.0 1.0 %copy-done = bf16[2,110592]{1,0:T(2,128)(2,1)S(1)} copy-done((bf16[2,110592]{1,0:T(2,128)(2,1)S(1)}, bf16[2,110592]{1,0:T(2,128)(2,1)}, u32[]{:S(2)}) %copy-start) | copy-done | bytes 442392
  1.0 0.0 copy-start.1
  1.0 0.7 %copy-done.1 = s32[1,2,1,6]{3,2,1,0:T(1,128)S(1)} copy-done((s32[1,2,1,6]{3,2,1,0:T(1,128)S(1)}, s32[1,2,1,6]{3,2,1,0:T(1,128)}, u32[]{:S(2)}) %copy-start.1) | copy-done | bytes 72
  1.7 0.8 %prepare.1 = (bf16[2,864,128]{2,1,0:T(8,128)(2,1)S(1)}, bf16[864,128]{1,0:T(8,128)(2,1)S(1)}, bf16[864,128]{1,0:T(8,128)(2,1)S(1)}, s32[1,2,1,6]{3,2,1,0:T(1,128)S(1)}) custom-call(s32[1,2,1,6]{3,2,1,0:T(1,128)S(1)} %copy-done.1, bf16[1728,128]{1,0:T(8,128)(2,1)S(1)} %bitcast.10), custom_call_target="tpu_custom_call" | custom-call | flops 1000000 | bytes 1000000 | tf_op jit(solution)/shard_map/prepare/pallas_call | solution.py:326
  2.5 6.5 %collective-permute-start.5 = (bf16[864,128]{1,0:T(8,128)(2,1)S(1)}, bf16[864,128]{1,0:T(8,128)(2,1)S(1)}, u32[]{:S(2)}, u32[]{:S(2)}) collective-permute-start(bf16[864,128]{1,0:T(8,128)(2,1)S(1)} %get-tuple-element.24), channel_id=1, source_target_pairs={{0,31},{1,0},{2,1},{3,2},{4,3},{5,4},{6,5},{7,6},{8,7},{9,8},{10,9... | collective-permute-start | bytes 663560 | tf_op jit(solution)/shard_map/ppermute | solution.py:423
  9.0 0.7 %collective-permute-start.2 = (s32[1,2,1,6]{3,2,1,0:T(1,128)S(1)}, s32[1,2,1,6]{3,2,1,0:T(1,128)S(1)}, u32[]{:S(2)}, u32[]{:S(2)}) collective-permute-start(s32[1,2,1,6]{3,2,1,0:T(1,128)S(1)} %copy-done.1), channel_id=1, source_target_pairs={{0,31},{1,0},{2,1},{3,2},{4,3},{5,4},{6,5},{7,6},{8,7},{9,8},{10,9... | collective-permute-start | bytes 152 | tf_op jit(solution)/shard_map/ppermute | solution.py:423
  9.6 0.5 %collective-permute-start.3 = (bf16[864,128]{1,0:T(8,128)(2,1)S(1)}, bf16[864,128]{1,0:T(8,128)(2,1)S(1)}, u32[]{:S(2)}, u32[]{:S(2)}) collective-permute-start(bf16[864,128]{1,0:T(8,128)(2,1)S(1)} %get-tuple-element.23), channel_id=1, source_target_pairs={{0,30},{1,31},{2,0},{3,1},{4,2},{5,3},{6,4},{7,5},{8,6},{9,7},{10,... | collective-permute-start | bytes 663560 | tf_op jit(solution)/shard_map/ppermute | solution.py:423
  10.2 4.5 %collective-permute-done.2.e_ref.refs_0_.e1_ref = s32[1,2,1,6]{3,2,1,0:T(1,128)S(1)} collective-permute-done((s32[1,2,1,6]{3,2,1,0:T(1,128)S(1)}, s32[1,2,1,6]{3,2,1,0:T(1,128)S(1)}, u32[]{:S(2)}, u32[]{:S(2)}) %collective-permute-start.2) | collective-permute-done | bytes 80 | tf_op jit(solution)/shard_map/ppermute | solution.py:423
  14.6 0.1 pick.3
  14.8 0.1 collective-permute-start.4
  14.8 6.0 %collective-permute-start = (s32[1,2,1,6]{3,2,1,0:T(1,128)S(1)}, s32[1,2,1,6]{3,2,1,0:T(1,128)S(1)}, u32[]{:S(2)}, u32[]{:S(2)}) collective-permute-start(s32[1,2,1,6]{3,2,1,0:T(1,128)S(1)} %copy-done.1), channel_id=1, source_target_pairs={{0,30},{1,31},{2,0},{3,1},{4,2},{5,3},{6,4},{7,5},{8,6},{9,7},{10,... | collective-permute-start | bytes 152 | tf_op jit(solution)/shard_map/ppermute | solution.py:423
  20.9 1.3 %collective-permute-done.e_ref.e2_ref = s32[1,2,1,6]{3,2,1,0:T(1,128)S(1)} collective-permute-done((s32[1,2,1,6]{3,2,1,0:T(1,128)S(1)}, s32[1,2,1,6]{3,2,1,0:T(1,128)S(1)}, u32[]{:S(2)}, u32[]{:S(2)}) %collective-permute-start) | collective-permute-done | bytes 80 | tf_op jit(solution)/shard_map/ppermute | solution.py:423
  22.2 0.1 pick.2
  22.3 0.1 collective-permute-start.1
  22.4 0.8 %tables.1 = (bf16[128,256]{1,0:T(8,128)(2,1)S(1)}, bf16[96,144]{1,0:T(8,128)(2,1)S(1)}, bf16[96,192]{1,0:T(8,128)(2,1)S(1)}, bf16[96,256]{1,0:T(8,128)(2,1)S(1)}, f32[48,96,128]{2,1,0:T(8,128)S(1)}) custom-call(), custom_call_target="tpu_custom_call" | custom-call | flops 10000000 | bytes 1000000 | tf_op jit(solution)/shard_map/tables/pallas_call | solution.py:356
  23.2 0.0 collective-permute-done.5.refs_2_
  23.2 2.6 %shard_map.28.refs_5_ = f32[18,48,128]{2,1,0:T(8,128)S(1)} custom-call(s32[1,2,1,6]{3,2,1,0:T(1,128)S(1)} %collective-permute-done.2.e_ref.refs_0_.e1_ref, bf16[2,864,128]{2,1,0:T(8,128)(2,1)S(1)} %get-tuple-element.17.w_ref.refs_1_, bf16[864,128]{1,0:T(8,128)(2,1)S(1)} %collective-permute-done.5.refs_2_, ...), custom_call_target="tpu_custom_call" | custom-call | flops 200000000 | bytes 4000000 | tf_op jit(solution)/shard_map/pallas_call | solution.py:406
  25.8 0.0 collective-permute-done.3.x1_ref
  25.9 0.0 collective-permute-done.4.x2_ref
  25.9 4.4 %solve_middle.1 = (f32[2,18,48,128]{3,2,1,0:T(8,128)S(1)}, f32[18,48,128]{2,1,0:T(8,128)S(1)}) custom-call(s32[1,2,1,6]{3,2,1,0:T(1,128)S(1)} %collective-permute-done.e_ref.e2_ref, s32[1,2,1,6]{3,2,1,0:T(1,128)S(1)} %collective-permute-done.2.e_ref.refs_0_.e1_ref, s32[1,2,1,6]{3,2,1,0:T(1,128)S(1)} %get-tuple-element.16.own_ref.refs_0_, ...), custom_call_target="tpu_custom_call" | custom-call | flops 400000000 | bytes 8000000 | tf_op jit(solution)/shard_map/solve_middle/pallas_call | solution.py:384
  30.3 2.4 %collective-permute-done.1.refs_2_ = bf16[864,128]{1,0:T(8,128)(2,1)S(1)} collective-permute-done((bf16[864,128]{1,0:T(8,128)(2,1)S(1)}, bf16[864,128]{1,0:T(8,128)(2,1)S(1)}, u32[]{:S(2)}, u32[]{:S(2)}) %collective-permute-start.1) | collective-permute-done | bytes 221216 | tf_op jit(solution)/shard_map/ppermute | solution.py:423
  32.7 3.3 %shard_map.29 = bf16[1728,128]{1,0:T(8,128)(2,1)} custom-call(s32[1,2,1,6]{3,2,1,0:T(1,128)S(1)} %get-tuple-element.16.own_ref.refs_0_, bf16[2,864,128]{2,1,0:T(8,128)(2,1)S(1)} %get-tuple-element.17.w_ref.refs_1_, bf16[864,128]{1,0:T(8,128)(2,1)S(1)} %collective-permute-done.1.refs_2_, bf16[128,256]{1,0:T(8,128)(2,1)S(1)} %get-tuple-element.18.refs_3_.refs_0_, ...), custom_call_target="tpu_custom_call" | custom-call | flops 200000000 | bytes 4000000 | tf_op jit(solution)/shard_map/pallas_call | solution.py:406
Async XLA Ops:
  0.0 1.0 %copy-start = (bf16[2,110592]{1,0:T(2,128)(2,1)S(1)}, bf16[2,110592]{1,0:T(2,128)(2,1)}, u32[]{:S(2)}) copy-start(bf16[2,110592]{1,0:T(2,128)(2,1)} %param.2) | copy-start | bytes 1327108
  1.0 0.7 %copy-start.1 = (s32[1,2,1,6]{3,2,1,0:T(1,128)S(1)}, s32[1,2,1,6]{3,2,1,0:T(1,128)}, u32[]{:S(2)}) copy-start(s32[1,2,1,6]{3,2,1,0:T(1,128)} %e_hbm.1) | copy-start | bytes 148
  2.5 20.7 %collective-permute-start.5 = (bf16[864,128]{1,0:T(8,128)(2,1)S(1)}, bf16[864,128]{1,0:T(8,128)(2,1)S(1)}, u32[]{:S(2)}, u32[]{:S(2)}) collective-permute-start(bf16[864,128]{1,0:T(8,128)(2,1)S(1)} %get-tuple-element.24), channel_id=1, source_target_pairs={{0,31},{1,0},{2,1},{3,2},{4,3},{5,4},{6,5},{7,6},{8,7},{9,8},{10,9... | collective-permute-start | bytes 663560 | tf_op jit(solution)/shard_map/ppermute | solution.py:423
  9.0 5.7 %collective-permute-start.2 = (s32[1,2,1,6]{3,2,1,0:T(1,128)S(1)}, s32[1,2,1,6]{3,2,1,0:T(1,128)S(1)}, u32[]{:S(2)}, u32[]{:S(2)}) collective-permute-start(s32[1,2,1,6]{3,2,1,0:T(1,128)S(1)} %copy-done.1), channel_id=1, source_target_pairs={{0,31},{1,0},{2,1},{3,2},{4,3},{5,4},{6,5},{7,6},{8,7},{9,8},{10,9... | collective-permute-start | bytes 152 | tf_op jit(solution)/shard_map/ppermute | solution.py:423
  9.6 16.2 %collective-permute-start.3 = (bf16[864,128]{1,0:T(8,128)(2,1)S(1)}, bf16[864,128]{1,0:T(8,128)(2,1)S(1)}, u32[]{:S(2)}, u32[]{:S(2)}) collective-permute-start(bf16[864,128]{1,0:T(8,128)(2,1)S(1)} %get-tuple-element.23), channel_id=1, source_target_pairs={{0,30},{1,31},{2,0},{3,1},{4,2},{5,3},{6,4},{7,5},{8,6},{9,7},{10,... | collective-permute-start | bytes 663560 | tf_op jit(solution)/shard_map/ppermute | solution.py:423
  14.8 11.1 %collective-permute-start.4 = (bf16[864,128]{1,0:T(8,128)(2,1)S(1)}, bf16[864,128]{1,0:T(8,128)(2,1)S(1)}, u32[]{:S(2)}, u32[]{:S(2)}) collective-permute-start(bf16[864,128]{1,0:T(8,128)(2,1)S(1)} %pick.3), channel_id=1, source_target_pairs={{0,1},{1,2},{2,3},{3,4},{4,5},{5,6},{6,7},{7,8},{8,9},{9,10},{10,1... | collective-permute-start | bytes 663560 | tf_op jit(solution)/shard_map/ppermute | solution.py:423
  14.8 7.3 %collective-permute-start = (s32[1,2,1,6]{3,2,1,0:T(1,128)S(1)}, s32[1,2,1,6]{3,2,1,0:T(1,128)S(1)}, u32[]{:S(2)}, u32[]{:S(2)}) collective-permute-start(s32[1,2,1,6]{3,2,1,0:T(1,128)S(1)} %copy-done.1), channel_id=1, source_target_pairs={{0,30},{1,31},{2,0},{3,1},{4,2},{5,3},{6,4},{7,5},{8,6},{9,7},{10,... | collective-permute-start | bytes 152 | tf_op jit(solution)/shard_map/ppermute | solution.py:423
  22.3 10.4 %collective-permute-start.1 = (bf16[864,128]{1,0:T(8,128)(2,1)S(1)}, bf16[864,128]{1,0:T(8,128)(2,1)S(1)}, u32[]{:S(2)}, u32[]{:S(2)}) collective-permute-start(bf16[864,128]{1,0:T(8,128)(2,1)S(1)} %pick.2), channel_id=1, source_target_pairs={{0,2},{1,3},{2,4},{3,5},{4,6},{5,7},{6,8},{7,9},{8,10},{9,11},{10,... | collective-permute-start | bytes 663560 | tf_op jit(solution)/shard_map/ppermute | solution.py:423
